TPU v7x, 256 devices: a whole 4x4x8 slice. The times are simulated.
256 devices in a mesh: ctx: 32 (over z, y), head: 8 (over x, core).
Axes of the slice: x: 4, y: 4, z: 8, core: 2. Of those that a mesh axis runs over, the one named last changes fastest.
Arguments:
- query: bfloat16 [32, 128, 576], P('ctx', 'head'), may hold values from -20 to 20
- cache: bfloat16 [131072, 576], P('ctx'), may hold values from -20 to 20
- cotangent: bfloat16 [32, 128, 512], P('ctx', 'head'), may hold values from -6 to 6
- positions: int32 [32], P('ctx'), may hold values from 0 to 262143
- visible: int32 [32], replicated, may hold values from 128 to 131072, as said below
Outputs:
- attention: bfloat16 [32, 128, 512], P('ctx', 'head')
- grad_query: float32 [32, 128, 576], P('ctx', 'head')
- grad_cache: bfloat16 [131072, 576], P('ctx')
Inputs may be any that keep to these rules, and one draw needn't show every extreme that they name: `visible`: each entry is a multiple of 128; some rollout token sees all 131072 prompt tokens.
All inputs are finite; a program needn't handle non-finite values.
Results may differ from a plain program's by a relative error of at most 0.01855.
Values may be sent and summed in bfloat16 or wider, within the bound.
A program may use at most 128 MiB of HBM per device.

v0:
```python
import jax
import jax.numpy as jnp
import numpy as np
from jax import lax
from jax.sharding import PartitionSpec as P

softmax_scale = 192.0 ** (-0.5)
position_bits = 18
masked_value = -1e30


def laid_out(parts, dim):
    parts = jnp.moveaxis(parts, 0, dim)
    lengths = parts.shape
    return parts.reshape(*lengths[:dim], lengths[dim] * lengths[dim + 1], *lengths[dim + 2 :])


def gather_packed(arrays, axis, dims):
    vector = jnp.concatenate([a.reshape(-1) for a in arrays])
    lines, at, gathered = (lax.all_gather(vector, axis), 0, [])
    for a, dim in zip(arrays, dims):
        parts = lines[:, at : at + a.size].reshape(-1, *a.shape)
        gathered.append(laid_out(parts, dim))
        at += a.size
    return tuple(gathered)


def from_everyone(value, axis):
    copies = jnp.broadcast_to(value, (lax.axis_size(axis), *value.shape))
    return lax.all_to_all(copies, axis, split_axis=0, concat_axis=0, tiled=True)


def over_copies(value, axis):
    return from_everyone(value, axis).max(axis=0)


def over_copies_2(value, axis):
    return from_everyone(value, axis).sum(axis=0)


def cut_along(value, dim, size):
    before, after = (value.shape[:dim], value.shape[dim + 1 :])
    return jnp.moveaxis(value.reshape(*before, size, -1, *after), dim, 0)


def sent_and_summed(value, axis, dim):
    parts = cut_along(value, dim, lax.axis_size(axis))
    arrived = lax.all_to_all(parts, axis, split_axis=0, concat_axis=0, tiled=True)
    return arrived.astype(jnp.float32).sum(axis=0)


def rotation(positions, half_width):
    frequency = 10000.0 ** (-np.arange(half_width) / half_width)
    angles = np.outer(2.0 ** np.arange(position_bits), frequency)
    cosine_table = jnp.asarray(np.cos(angles), jnp.float32)
    sine_table = jnp.asarray(np.sin(angles), jnp.float32)
    cosines = jnp.ones((positions.shape[0], half_width), jnp.float32)
    sine_part = jnp.zeros((positions.shape[0], half_width), jnp.float32)
    for bit_index in range(position_bits):
        switch = (positions // 2**bit_index % 2).astype(jnp.float32)[:, None]
        step_cos = 1.0 + switch * (cosine_table[bit_index] - 1.0)
        step_sin = switch * sine_table[bit_index]
        cosines, sine_part = (
            cosines * step_cos - sine_part * step_sin,
            sine_part * step_cos + cosines * step_sin,
        )
    return (cosines[:, None, :], sine_part[:, None, :])


def rotate(tensor, cosines, sine_part, value_width, inverse):
    half_width = cosines.shape[-1]
    lower = tensor[..., value_width : value_width + half_width]
    upper = tensor[..., value_width + half_width :]
    if inverse:
        sine_part = -sine_part
    new_lower = lower * cosines - upper * sine_part
    new_upper = lower * sine_part + upper * cosines
    return jnp.concatenate([tensor[..., :value_width], new_lower, new_upper], axis=-1)


def body(query, cache, cotangent, positions, visible):
    value_width = cotangent.shape[-1]
    half_width = (query.shape[-1] - value_width) // 2
    extra_width = cache.shape[1] - value_width
    cosines, sine_part = rotation(positions, half_width)
    rotated = rotate(query.astype(jnp.float32), cosines, sine_part, value_width, False).astype(
        jnp.bfloat16
    )
    rotated, gradients = gather_packed((rotated, cotangent), "ctx", (0, 0))
    block_rows = cache.shape[0]
    first_key = lax.axis_index("ctx") * block_rows
    key_index = first_key + jnp.arange(block_rows)
    allowed = key_index[None, None, :] < visible[:, None, None]
    scores = (
        jnp.einsum("thl,kl->thk", rotated, cache, preferred_element_type=jnp.float32)
        * softmax_scale
    )
    scores = jnp.where(allowed, scores, masked_value)
    local_peak = jnp.max(scores, axis=2)
    peak = over_copies(local_peak, "ctx")
    weights = jnp.where(allowed, jnp.exp(scores - peak[..., None]), 0.0)
    local_mass = jnp.sum(weights, axis=2)
    mass = over_copies_2(local_mass, "ctx")
    probs = weights / mass[..., None]
    prob_low = probs.astype(jnp.bfloat16)
    values = cache[:, :value_width]
    attended = jnp.einsum("thk,kv->thv", prob_low, values, preferred_element_type=jnp.float32)
    attention = sent_and_summed(attended.astype(jnp.bfloat16), "ctx", 0).astype(jnp.bfloat16)
    grad_probs = jnp.einsum("thv,kv->thk", gradients, values, preferred_element_type=jnp.float32)
    local_delta = jnp.sum(prob_low.astype(jnp.float32) * grad_probs, axis=2)
    delta = over_copies_2(local_delta, "ctx")
    grad_scores = (probs * (grad_probs - delta[..., None]) * softmax_scale).astype(jnp.bfloat16)
    grad_rotated = jnp.einsum("thk,kl->thl", grad_scores, cache, preferred_element_type=jnp.float32)
    grad_latent = jnp.einsum(
        "thk,thl->kl", grad_scores, rotated, preferred_element_type=jnp.float32
    )
    grad_value = jnp.einsum("thk,thv->kv", prob_low, gradients, preferred_element_type=jnp.float32)
    grad_latent = grad_latent + jnp.pad(grad_value, ((0, 0), (0, extra_width)))
    grad_cache = lax.psum(grad_latent, "head").astype(jnp.bfloat16)
    grad_rotated = sent_and_summed(grad_rotated.astype(jnp.bfloat16), "ctx", 0)
    grad_query = rotate(grad_rotated, cosines, sine_part, value_width, True)
    return (attention, grad_query, grad_cache)


def solution(mesh):
    placed = (P("ctx", "head", None), P("ctx", None), P("ctx", "head", None), P("ctx"), P())
    return jax.shard_map(
        body,
        mesh=mesh,
        in_specs=placed,
        out_specs=(P("ctx", "head", None), P("ctx", "head", None), P("ctx", None)),
        check_vma=False,
    )
```

profile of v0, /device:TPU:1, one launch (start us, length us, event | category | flops | bytes accessed | tf_op | source)
XLA Modules:
  0.0 325.5 jit_solution(17583877375646782766)
XLA Ops:
  14.9 0.7 fusion.51
  18.8 0.8 broadcast_compare_fusion
  19.6 74.6 %all-gather.3.cloned.1.call-done = bf16[557056]{0:T(1024)(128)(2,1)} async-done(((bf16[17408]{0:T(1024)(128)(2,1)}), bf16[557056]{0:T(1024)(128)(2,1)}) %all-gather.3.cloned.1.call-update) | async-done | bytes 1114128 | tf_op jit(solution)/shard_map/all_gather | solution.py:20
  94.1 1.6 reshape.281
  96.3 8.4 %fusion = (f32[32,16]{1,0:T(8,128)S(1)}, f32[32,16,4096]{2,1,0:T(8,128)}) fusion(pred[32,4096]{1,0:T(8,128)(4,1)S(1)} %broadcast_compare_fusion, bf16[32,16,576]{2,1,0:T(8,128)(2,1)S(1)} %reshape_reshape.6, bf16[4096,576]{0,1:T(8,128)(2,1)} %param.8), kind=kOutput, calls=%fused_computation.5 | convolution fusion | flops 2422210048 | bytes 13830144 | tf_op jit(solution)/shard_map/thl,kl->thk/dot_general | solution.py:95
  104.9 14.7 %all_to_all.25 = f32[32,1,512]{2,1,0:T(1,128)S(1)} all-to-all(f32[32,1,512]{2,1,0:T(1,128)S(1)} %reshape.286), channel_id=1, replica_groups=mesh['ctx'=32,'head'=8] {'ctx'}, dimensions={0} | all-to-all | bytes 131072 | tf_op jit(solution)/shard_map/all_to_all | solution.py:30
  120.1 0.8 reduce.3
  121.2 5.0 %fusion.2 = f32[32,16]{1,0:T(8,128)S(1)} fusion(f32[32,16,4096]{2,1,0:T(8,128)} %get-tuple-element.37, f32[32,16]{1,0:T(8,128)S(1)} %copy.23, pred[32,4096]{1,0:T(8,128)(4,1)S(1)} %broadcast_compare_fusion), kind=kLoop, calls=%fused_computation.8 | loop fusion | flops 10485248 | bytes 8523776 | tf_op jit(solution)/shard_map/reduce_sum | solution.py:102
  126.3 0.8 reshape.288
  127.0 3.9 %all-to-all-start.1 = ((f32[32,1,512]{2,1,0:T(1,128)}), f32[32,1,512]{2,1,0:T(1,128)S(1)}, u32[]{:S(2)}, u32[]{:S(2)}) async-start(f32[32,1,512]{2,1,0:T(1,128)} %reshape.288), calls=%async_computation.1 | async-start | bytes 131072 | tf_op jit(solution)/shard_map/all_to_all | solution.py:30
  131.1 8.7 %all-to-all-done.1 = f32[32,1,512]{2,1,0:T(1,128)S(1)} async-done(((f32[32,1,512]{2,1,0:T(1,128)}), f32[32,1,512]{2,1,0:T(1,128)S(1)}, u32[]{:S(2)}, u32[]{:S(2)}) %all-to-all-start.1) | async-done | bytes 65568 | tf_op jit(solution)/shard_map/all_to_all | solution.py:30
  139.8 0.8 reduce.4
  140.8 10.3 %multiply_reduce_fusion = (f32[32,16]{1,0:T(8,128)S(1)}, bf16[32,16,4096]{2,1,0:T(8,128)(2,1)}, f32[32,16,4096]{2,1,0:T(8,128)}) fusion(f32[32,16]{1,0:T(8,128)S(1)} %copy.25, f32[32,16]{1,0:T(8,128)S(1)} %copy.23, f32[32,16,4096]{2,1,0:T(8,128)} %get-tuple-element.37, pred[32,4096]{1,0:T(8,128)(4,1)S(1)} %broadcast_compare_fusion, ...), kind=kOutput, calls=%fused_computation.2 | convolution fusion | flops 2166357504 | bytes 25827328 | tf_op jit(solution)/shard_map/thv,kv->thk/dot_general | solution.py:109
  151.2 0.8 reshape.290
  152.0 4.0 %all-to-all-start.3 = ((f32[32,1,512]{2,1,0:T(1,128)}), f32[32,1,512]{2,1,0:T(1,128)S(1)}, u32[]{:S(2)}, u32[]{:S(2)}) async-start(f32[32,1,512]{2,1,0:T(1,128)} %reshape.290), calls=%async_computation.3 | async-start | bytes 131072 | tf_op jit(solution)/shard_map/all_to_all | solution.py:30
  156.1 6.8 %fusion.22 = bf16[32,1,16,512]{3,2,1,0:T(8,128)(2,1)} fusion(bf16[32,16,4096]{2,1,0:T(8,128)(2,1)} %get-tuple-element.8, bf16[4096,576]{0,1:T(8,128)(2,1)} %param.8), kind=kOutput, calls=%fused_computation.23 | convolution fusion | flops 2147745792 | bytes 8912896 | tf_op jit(solution)/shard_map/thk,kv->thv/dot_general | solution.py:107
  162.9 5.7 %convolution_bitcast_fusion = f32[4096,512]{0,1:T(8,128)} fusion(bf16[32,16,4096]{2,1,0:T(8,128)(2,1)S(1)} %copy-done, bf16[32,16,512]{2,1,0:T(8,128)(2,1)S(1)} %bitcast.87), kind=kOutput, calls=%fused_computation.6 | convolution fusion | flops 2147483648 | bytes 13107200 | tf_op jit(solution)/shard_map/thk,thv->kv/dot_general | solution.py:117
  168.6 9.0 %all-to-all-start.2 = ((bf16[32,1,16,512]{3,2,1,0:T(8,128)(2,1)}), bf16[32,1,16,512]{3,2,1,0:T(8,128)(2,1)S(1)}, u32[]{:S(2)}, u32[]{:S(2)}) async-start(bf16[32,1,16,512]{3,2,1,0:T(8,128)(2,1)} %fusion.22), calls=%async_computation.2 | async-start | bytes 1048576 | tf_op jit(solution)/shard_map/all_to_all | solution.py:48
  177.6 0.8 reduce.5
  178.7 8.0 %multiply_convert_fusion = bf16[32,16,4096]{2,1,0:T(8,128)(2,1)S(1)} fusion(f32[32,16,4096]{2,1,0:T(8,128)} %get-tuple-element.38, f32[32,16]{1,0:T(8,128)S(1)} %copy.29, f32[32,16]{1,0:T(8,128)S(1)} %copy.25, f32[32,16]{1,0:T(8,128)S(1)} %copy.23, f32[32,16,4096]{2,1,0:T(8,128)} %get-tuple-element.37, pred[32,4096]{1,0:T(8,128)(4,1)S(1)} %broadcast_compare_fusion), kind=kLoop, calls=%fused_computation.1 | loop fusion | flops 18874368 | bytes 21108736 | tf_op jit(solution)/shard_map/convert_element_type | solution.py:112
  186.7 7.4 %bitcast_add_fusion = f32[4096,576]{0,1:T(8,128)} fusion(f32[4096,512]{0,1:T(8,128)} %convolution_bitcast_fusion, bf16[32,16,4096]{2,1,0:T(8,128)(2,1)S(1)} %multiply_convert_fusion, bf16[32,16,576]{2,1,0:T(8,128)(2,1)S(1)} %reshape_reshape.6), kind=kOutput, calls=%fused_computation | convolution fusion | flops 2418278400 | bytes 22609920 | tf_op jit(solution)/shard_map/thk,thl->kl/dot_general | solution.py:114
  194.1 4.3 %fusion.19 = bf16[32,1,16,576]{3,2,1,0:T(8,128)(2,1)} fusion(bf16[32,16,4096]{2,1,0:T(8,128)(2,1)S(1)} %multiply_convert_fusion, bf16[4096,576]{0,1:T(8,128)(2,1)S(1)} %bitcast.94), kind=kOutput, calls=%fused_computation.22 | convolution fusion | flops 2416214016 | bytes 9502720 | tf_op jit(solution)/shard_map/thk,kl->thl/dot_general | solution.py:113
  198.4 9.2 %all-to-all-start.4 = ((bf16[32,1,16,576]{3,2,1,0:T(8,128)(2,1)}), bf16[32,1,16,576]{3,2,1,0:T(8,128)(2,1)S(1)}, u32[]{:S(2)}, u32[]{:S(2)}) async-start(bf16[32,1,16,576]{3,2,1,0:T(8,128)(2,1)} %fusion.19), calls=%async_computation.4 | async-start | bytes 1310720 | tf_op jit(solution)/shard_map/all_to_all | solution.py:48
  207.6 109.4 %all-reduce.2 = bf16[4096,576]{0,1:T(8,128)(2,1)} all-reduce(f32[4096,576]{0,1:T(8,128)} %bitcast_add_fusion), channel_id=1, replica_groups=mesh['ctx'=32,'head'=8] {'head'}, use_global_device_ids=true, to_apply=%region_8.9 | all-reduce | flops 2359296 | bytes 14155776 | tf_op jit(solution)/shard_map/psum | solution.py:119
  (55 shorter events, 13.7 us)
Async XLA Ops:
  7.2 87.0 %all-gather.3.cloned.1.call-start = ((), (), s32[]{:S(2)}) async-start(), calls=%async_computation.5 | async-start | bytes 1148928 | tf_op jit(solution)/shard_map/all_gather | solution.py:20
  127.0 12.7 %all-to-all-start.1 = ((f32[32,1,512]{2,1,0:T(1,128)}), f32[32,1,512]{2,1,0:T(1,128)S(1)}, u32[]{:S(2)}, u32[]{:S(2)}) async-start(f32[32,1,512]{2,1,0:T(1,128)} %reshape.288), calls=%async_computation.1 | async-start | bytes 131072 | tf_op jit(solution)/shard_map/all_to_all | solution.py:30
  152.0 16.6 %all-to-all-start.3 = ((f32[32,1,512]{2,1,0:T(1,128)}), f32[32,1,512]{2,1,0:T(1,128)S(1)}, u32[]{:S(2)}, u32[]{:S(2)}) async-start(f32[32,1,512]{2,1,0:T(1,128)} %reshape.290), calls=%async_computation.3 | async-start | bytes 131072 | tf_op jit(solution)/shard_map/all_to_all | solution.py:30
  156.0 6.8 %copy-start = (bf16[32,16,4096]{2,1,0:T(8,128)(2,1)S(1)}, bf16[32,16,4096]{2,1,0:T(8,128)(2,1)}, u32[]{:S(2)}) copy-start(bf16[32,16,4096]{2,1,0:T(8,128)(2,1)} %get-tuple-element.8) | copy-start | bytes 12582916
  168.6 29.8 %all-to-all-start.2 = ((bf16[32,1,16,512]{3,2,1,0:T(8,128)(2,1)}), bf16[32,1,16,512]{3,2,1,0:T(8,128)(2,1)S(1)}, u32[]{:S(2)}, u32[]{:S(2)}) async-start(bf16[32,1,16,512]{3,2,1,0:T(8,128)(2,1)} %fusion.22), calls=%async_computation.2 | async-start | bytes 1048576 | tf_op jit(solution)/shard_map/all_to_all | solution.py:48
  178.7 15.4 %slice-start = ((s8[4718592]{0:T(1024)(128)(4,1)}), s8[4194304]{0:T(1024)(128)(4,1)S(1)}, s32[]{:S(2)}) async-start(s8[4718592]{0:T(1024)(128)(4,1)} %bitcast.93), calls=%async_computation.6 | async-start | bytes 8388608
  186.7 7.4 %slice-start.1 = ((s8[4718592]{0:T(1024)(128)(4,1)}), s8[524288]{0:T(1024)(128)(4,1)S(1)}, s32[]{:S(2)}) async-start(s8[4718592]{0:T(1024)(128)(4,1)} %bitcast.93), calls=%async_computation.7 | async-start | bytes 1048576
  198.4 119.3 %all-to-all-start.4 = ((bf16[32,1,16,576]{3,2,1,0:T(8,128)(2,1)}), bf16[32,1,16,576]{3,2,1,0:T(8,128)(2,1)S(1)}, u32[]{:S(2)}, u32[]{:S(2)}) async-start(bf16[32,1,16,576]{3,2,1,0:T(8,128)(2,1)} %fusion.19), calls=%async_computation.4 | async-start | bytes 1310720 | tf_op jit(solution)/shard_map/all_to_all | solution.py:48
Sparse Core Ops, SparseCore 0:
  18.9 75.2 all-gather.2
where the time goes:
time: 326 us; the launch traced here: 325 us
  blocking collectives  124 us (38%)
  waiting for transfers between devices  83.2 us (26%)
  matrix products  42.9 us (13%)
  other arithmetic  26.7 us (8%)
  starting transfers between devices  26.2 us (8%)
  between operations  15.3 us (5%)
  local copies, waits for them, and re-layouts  6.96 us (2%)
    psum x1, blocking collectives, body(): grad_cache = lax.psum(grad_latent, 'head').astype(jnp.bfloat16)  109 us
    all_gather x1, waiting for transfers between devices, gather_packed(): lines, at, gathered = (lax.all_gather(vector, axis), 0, [])  74.6 us
    all_to_all x2, starting transfers between devices, sent_and_summed(): lax.all_to_all(parts, axis, split_axis=0, concat_axis=0, tiled=True)  18.3 us
    all_to_all x1, blocking collectives, from_everyone(): return lax.all_to_all(copies, axis, split_axis=0, concat_axis=0, tiled=True)  14.7 us
    dot_general x1, matrix products, body(): jnp.einsum('thv,kv->thk', gradients, values, preferred_element_type=jnp.f...  10.3 us
    all_to_all x2, waiting for transfers between devices, from_everyone(): return lax.all_to_all(copies, axis, split_axis=0, concat_axis=0, tiled=True)  8.66 us
    dot_general x1, matrix products, body(): jnp.einsum('thl,kl->thk', rotated, cache, preferred_element_type=jnp.floa...  8.4 us
    convert_element_type x1, other arithmetic, body(): (probs * (grad_probs - delta[..., None]) * softmax_scale).astype(jnp.bflo...  7.99 us
  transfers between devices with their start and end apart: 5, of which 2 were waited for; matrix products, arithmetic and copies ran while one was open for 11% of the time, Pallas kernels for 0%

commit v1 on v0

v1 whole, which is shorter than its diff:
```python
import jax
import jax.numpy as jnp
import numpy as np
from jax import lax
from jax.experimental import pallas as pl
from jax.experimental.pallas import tpu as pltpu
from jax.sharding import PartitionSpec as P

softmax_scale = 192.0 ** (-0.5)
log2_scale = softmax_scale * float(np.log2(np.e))
position_bits = 18
masked_value = -1e30

SZ, SY, SX = 8, 4, 4
CTX, HEAD = SZ * SY, SX * 2
F32, BF16 = jnp.float32, jnp.bfloat16
MESH = pl.DeviceIdType.MESH


def remote(src, dst, send_sem, recv_sem, device):
    return pltpu.make_async_remote_copy(
        src_ref=src,
        dst_ref=dst,
        send_sem=send_sem,
        recv_sem=recv_sem,
        device_id=device,
        device_id_type=MESH,
    )


def rows8(value, op):
    groups = value.reshape(value.shape[0] // 8, 8, value.shape[1])
    return op(groups, axis=0)


def kernel(
    vis_ref, pos_ref, cos_ref, sin_ref, query_ref, cot_ref, cache_ref,
    att_ref, gq_ref, gc_ref,
    qb, dob, keys, keys_t, q_t, do_t, qdo, scores, gprobs, low, grads,
    stat_own, stat_y, stat_z, acc, dd_out, dd_in, opp_out, opp_in, rs_out, rs_in,
    att_out, att_in, gq_out, gq_in,
    cache_sem, qy_s, qy_r, qz_s, qz_r, dz_s, dz_r, dy_s, dy_r,
    sy_s, sy_r, sz_s, sz_r, dd_s, dd_r, op_s, op_r, rs_s, rs_r,
    ag_s, ag_r, fw_s, fw_r, pp_s, pp_r, out_sem, at_s, at_r, gq_s, gq_r,
):
    ctx = lax.axis_index("ctx")
    head = lax.axis_index("head")
    z, y = ctx // SY, ctx % SY
    x, core = head // 2, head % 2
    n_keys = keys.shape[0]
    vd = cot_ref.shape[1]
    width = query_ref.shape[1]
    per = query_ref.shape[0]
    rows = CTX * per
    own_keys = n_keys // HEAD
    wave_keys = own_keys // 2
    half_keys = wave_keys // 2
    sends = []

    def plane(zz, yy):
        return (zz % SZ) * SY + yy % SY, head

    right = (ctx, ((x + 1) % SX) * 2 + core)
    left = (ctx, ((x + SX - 1) % SX) * 2 + core)
    partner = (ctx, x * 2 + 1 - core)

    def send(*args):
        copy = remote(*args)
        copy.start()
        sends.append(copy)

    def arrive(dst, send_sem, recv_sem, device):
        remote(dst, dst, send_sem, recv_sem, device).wait_recv()

    load = pltpu.make_async_copy(cache_ref, keys, cache_sem)
    load.start()

    barrier = pltpu.get_barrier_semaphore()

    def greet(k, carry):
        pl.semaphore_signal(
            barrier, inc=1, device_id=((ctx + k) % CTX, head), device_id_type=MESH
        )
        return carry

    lax.fori_loop(1, CTX, greet, 0)
    for device in (right, left, partner):
        pl.semaphore_signal(barrier, inc=1, device_id=device, device_id_type=MESH)

    position = pos_ref[0]
    half = (width - vd) // 2
    cosines = jnp.ones((1, 2 * half), F32)
    sines = jnp.zeros((1, 2 * half), F32)
    for bit in range(position_bits):
        switch = ((position >> bit) & 1).astype(F32)
        step_cos = 1.0 + switch * (cos_ref[bit : bit + 1, :] - 1.0)
        step_sin = switch * sin_ref[bit : bit + 1, :]
        cosines, sines = (
            cosines * step_cos - sines * step_sin,
            sines * step_cos + cosines * step_sin,
        )
    lower = lax.broadcasted_iota(jnp.int32, (1, 2 * half), 1) < half
    signed = jnp.where(lower, -sines, sines)

    def swapped(t):
        return jnp.concatenate([t[:, half:], t[:, :half]], axis=1)

    rotary = query_ref[:, vd:].astype(F32)
    qb[z, y, :, :vd] = query_ref[:, :vd]
    qb[z, y, :, vd:] = (rotary * cosines + swapped(rotary) * signed).astype(BF16)
    dob[z, y] = cot_ref[...]

    lane = lax.broadcasted_iota(jnp.int32, (1, rows), 1) // per
    seen = jnp.zeros((1, rows), jnp.int32)
    for t in range(CTX):
        seen = jnp.where(lane == t, vis_ref[t], seen)

    pl.semaphore_wait(barrier, CTX - 1 + 3)

    for d in range(1, SY):
        send(qb.at[z, y], qb.at[z, y], qy_s.at[d], qy_r.at[d], plane(z, y + d))
    for d in range(1, SZ):
        send(dob.at[z, y], dob.at[z, y], dz_s.at[d], dz_r.at[d], plane(z + d, y))

    def ring(way, step, d):
        sign = 1 if way == 0 else -1
        zz = (z - sign * (step - 1) + SZ) % SZ
        yy = (y - d + SY) % SY
        at = (way * (SZ // 2) + step - 1) * SY + d
        block = qb.at[zz, yy]
        send(block, block, qz_s.at[at], qz_r.at[at], plane(z + sign + SZ, y))

    def ring_arrive(way, step, d):
        sign = 1 if way == 0 else -1
        zz = (z - sign * step + SZ) % SZ
        yy = (y - d + SY) % SY
        at = (way * (SZ // 2) + step - 1) * SY + d
        arrive(qb.at[zz, yy], qz_s.at[at], qz_r.at[at], plane(z + sign + SZ, y))

    def carried(way, step, d):
        return step < SZ // 2 or (d < SY // 2) == (way == 0)

    n_t = 8
    t_keys = n_keys // n_t

    def transpose_keys(i):
        at = i * t_keys
        keys_t[:, at : at + t_keys] = keys[at : at + t_keys, :].T

    for d in range(SY):
        if d:
            src = qb.at[z, (y - d + SY) % SY]
            arrive(src, qy_s.at[d], qy_r.at[d], plane(z, y + d))
        ring(0, 1, d)
        ring(1, 1, d)
        if d == 0:
            load.wait()
            transpose_keys(0)
    for step in range(1, SZ // 2 + 1):
        transpose_keys(2 * step - 1)
        if 2 * step < n_t:
            transpose_keys(2 * step)
        for d in range(SY):
            for way in range(2):
                if carried(way, step, d):
                    ring_arrive(way, step, d)
                    if step < SZ // 2 and carried(way, step + 1, d):
                        ring(way, step + 1, d)
        if step == 2:
            for d in range(1, SZ):
                src = dob.at[(z - d + SZ) % SZ, y]
                arrive(src, dz_s.at[d], dz_r.at[d], plane(z + d, y))
            for d in range(1, SY):
                src = dob.at[:, y]
                send(src, src, dy_s.at[d], dy_r.at[d], plane(z, y + d))

    q_all = qb[...].reshape(rows, width)
    q_t[...] = q_all.T
    qdo[:rows, :] = q_all[:, :vd]
    chunk = 256
    n_chunks = n_keys // chunk
    first_key = ctx * n_keys

    def score(i, top):
        at = pl.multiple_of(i * chunk, chunk)
        raw = jnp.dot(keys[pl.ds(at, chunk), :], q_t[...], preferred_element_type=F32)
        base = first_key + at
        for part in range(chunk // 128):
            bias = jnp.where(base + part * 128 < seen, 0.0, masked_value).astype(F32)
            piece = raw[part * 128 : (part + 1) * 128, :] * log2_scale + bias
            scores[pl.ds(pl.multiple_of(at + part * 128, 128), 128), :] = piece
            top = jnp.maximum(top, rows8(piece, jnp.max))
        return top

    top = lax.fori_loop(0, n_chunks, score, jnp.full((8, rows), 2 * masked_value, F32))
    peak = jnp.max(top, axis=0, keepdims=True)

    for d in range(1, SY):
        src = dob.at[:, (y - d + SY) % SY]
        arrive(src, dy_s.at[d], dy_r.at[d], plane(z, y + d))
    do_all = dob[...].reshape(rows, vd)
    do_t[...] = do_all.T
    qdo[rows:, :] = do_all

    def weigh(i, sums):
        mass, inner = sums
        at = pl.multiple_of(i * chunk, chunk)
        window = pl.ds(at, chunk)
        weights = jnp.exp2(scores[window, :] - peak)
        gp = jnp.dot(keys[window, :vd], do_t[...], preferred_element_type=F32)
        scores[window, :] = weights
        gprobs[window, :] = gp
        low[window, :] = weights.astype(BF16)
        return mass + rows8(weights, jnp.sum), inner + rows8(weights * gp, jnp.sum)

    zero = jnp.zeros((8, rows), F32)
    mass, inner = lax.fori_loop(0, n_chunks, weigh, (zero, zero))
    mass = jnp.sum(mass, axis=0, keepdims=True)
    inner = jnp.sum(inner, axis=0, keepdims=True)

    n_lines = rows // 128

    def put_stats(ref, stats):
        for k, stat in enumerate(stats):
            for i in range(n_lines):
                ref[k * n_lines + i : k * n_lines + i + 1, :] = stat[:, i * 128 : (i + 1) * 128]

    def merge(parts):
        tops = [p[:n_lines] for p in parts]
        best = tops[0]
        for t in tops[1:]:
            best = jnp.maximum(best, t)
        total, dots = 0.0, 0.0
        for t, p in zip(tops, parts):
            factor = jnp.exp2(t - best)
            total = total + factor * p[n_lines : 2 * n_lines]
            dots = dots + factor * p[2 * n_lines : 3 * n_lines]
        return best, total, dots

    put_stats(stat_own, (peak, mass, inner, jnp.zeros_like(peak)))
    for d in range(1, SY):
        send(stat_own, stat_y.at[d], sy_s.at[d], sy_r.at[d], plane(z, y + d))
    first = jnp.dot(keys_t[:vd, :], low[:, : rows // 2], preferred_element_type=F32)
    for d in range(1, SY):
        arrive(stat_y.at[d], sy_s.at[d], sy_r.at[d], plane(z, y + d))
    best, total, dots = merge([stat_own[...]] + [stat_y[d] for d in range(1, SY)])
    stat_z[0, :n_lines] = best
    stat_z[0, n_lines : 2 * n_lines] = total
    stat_z[0, 2 * n_lines : 3 * n_lines] = dots
    stat_z[0, 3 * n_lines :] = jnp.zeros_like(dots)
    for d in range(1, SZ):
        send(stat_z.at[0], stat_z.at[d], sz_s.at[d], sz_r.at[d], plane(z + d, y))
    second = jnp.dot(keys_t[:vd, :], low[:, rows // 2 :], preferred_element_type=F32)
    att_t = jnp.concatenate([first, second], axis=1)
    for d in range(1, SZ):
        arrive(stat_z.at[d], sz_s.at[d], sz_r.at[d], plane(z + d, y))
    best, total, dots = merge([stat_z[d] for d in range(SZ)])

    def across(v):
        return jnp.concatenate([v[i : i + 1, :] for i in range(n_lines)], axis=1)

    factor = jnp.exp2(peak - across(best)) / across(total)
    delta = across(dots) / across(total)

    att_out[...] = (att_t * factor).T.astype(BF16).reshape(CTX, per, vd)

    def send_att(k, carry):
        to = (ctx + k) % CTX
        remote(att_out.at[to], att_in.at[k], at_s.at[k], at_r.at[k], (to, head)).start()
        return carry

    lax.fori_loop(1, CTX, send_att, 0)

    def spot(xx, cc, wave):
        return pl.multiple_of((xx * 2 + cc) * own_keys + wave * wave_keys, wave_keys)

    def terms(at):
        window = pl.ds(at, wave_keys)
        probs = scores[window, :] * factor
        grad = (probs * (gprobs[window, :] - delta) * softmax_scale).astype(BF16)
        grads[window, :] = grad
        both = jnp.concatenate([grad, probs.astype(BF16)], axis=1)
        value = jnp.dot(both, qdo[...], preferred_element_type=F32)
        q_rotary = qb[...].reshape(rows, width)[:, vd:]
        return value, jnp.dot(grad, q_rotary, preferred_element_type=F32)

    offsets = (2, 1, 3, 0)
    halves = (slice(0, half_keys), slice(half_keys, 2 * half_keys))

    def chip_sum(wave, slot, part):
        at = wave * 4 + slot
        return acc[at, part, :] + dd_in[at, part, :].astype(F32)

    def start_wave(wave):
        for slot, offset in enumerate(offsets):
            at = wave * 4 + slot
            xx = (x + offset) % SX
            value, rotary_part = terms(spot(xx, 1 - core, wave))
            dd_out[at, :, :vd] = value.astype(BF16)
            dd_out[at, :, vd:] = rotary_part.astype(BF16)
            send(dd_out.at[at], dd_in.at[at], dd_s.at[at], dd_r.at[at], partner)
            value, rotary_part = terms(spot(xx, core, wave))
            acc[at, :, :vd] = value
            acc[at, :, vd:] = rotary_part
            arrive(dd_in.at[at], dd_s.at[at], dd_r.at[at], partner)
            if slot == 0:
                for h, device in ((0, right), (1, left)):
                    opp_out[wave, h] = chip_sum(wave, 0, halves[h]).astype(BF16)
                    k = wave * 2 + h
                    send(opp_out.at[wave, h], opp_in.at[wave, h], op_s.at[k], op_r.at[k], device)
            if slot == 1:
                send_rs(wave, 0, 1, None)
            if slot == 2:
                send_rs(wave, 1, 0, None)

    def send_rs(wave, way, h, extra):
        part = chip_sum(wave, 1 + way, halves[h])
        if extra is not None:
            part = part + extra.astype(F32)
        rs_out[wave, way, h] = part.astype(BF16)
        k = (wave * 2 + way) * 2 + h
        device = (right, left)[way]
        send(rs_out.at[wave, way, h], rs_in.at[wave, way, h], rs_s.at[k], rs_r.at[k], device)

    def relay_wave(wave):
        for h, device in ((0, right), (1, left)):
            k = wave * 2 + h
            arrive(opp_in.at[wave, h], op_s.at[k], op_r.at[k], device)
            send_rs(wave, h, h, opp_in[wave, h])

    gc = gc_ref
    landed = []

    def piece(xx, cc, wave, h):
        at = (xx * 2 + cc) * own_keys + wave * wave_keys + h * half_keys
        return pl.ds(pl.multiple_of(at, half_keys), half_keys)

    def write_out(xx, cc, wave, h):
        at = piece(xx, cc, wave, h)
        k = len(landed)
        copy = pltpu.make_async_copy(full.at[at, :], gc.at[at, :], out_sem.at[k])
        copy.start()
        landed.append(copy)

    full = keys

    def finish_wave(wave):
        for h in range(2):
            for way in range(2):
                k = (wave * 2 + way) * 2 + h
                arrive(rs_in.at[wave, way, h], rs_s.at[k], rs_r.at[k], (right, left)[way])
        for h in range(2):
            done = chip_sum(wave, 3, halves[h])
            done = done + rs_in[wave, 0, h].astype(F32) + rs_in[wave, 1, h].astype(F32)
            full[piece(x, core, wave, h), :] = done.astype(BF16)
        for h, way in ((0, 0), (1, 1), (1, 0), (0, 1)):
            src = full.at[piece(x, core, wave, h), :]
            k = (wave * 2 + way) * 2 + h
            send(src, src, ag_s.at[k], ag_r.at[k], (right, left)[way])
        for h in range(2):
            to_partner(0, x, wave, h)
            write_out(x, core, wave, h)

    def to_partner(kind, xx, wave, h):
        src = full.at[piece(xx, core, wave, h), :]
        k = (kind * 2 + wave) * 2 + h
        send(src, src, pp_s.at[k], pp_r.at[k], partner)

    def from_side(wave, way, h):
        xx = (x + (SX - 1 if way == 0 else 1)) % SX
        here = full.at[piece(xx, core, wave, h), :]
        k = (wave * 2 + way) * 2 + h
        arrive(here, ag_s.at[k], ag_r.at[k], (right, left)[way])
        if h == way:
            k = wave * 2 + way
            send(here, here, fw_s.at[k], fw_r.at[k], (right, left)[way])
        to_partner(1 + way, xx, wave, h)
        write_out(xx, core, wave, h)

    def from_far(wave, way):
        xx = (x + 2) % SX
        here = full.at[piece(xx, core, wave, way), :]
        k = wave * 2 + way
        arrive(here, fw_s.at[k], fw_r.at[k], (right, left)[way])
        to_partner(3, xx, wave, way)
        write_out(xx, core, wave, way)

    def from_partner(wave):
        for kind, offset in enumerate((0, 3, 1, 2)):
            for h in range(2):
                xx = (x + offset) % SX
                here = full.at[piece(xx, 1 - core, wave, h), :]
                k = (kind * 2 + wave) * 2 + h
                arrive(here, pp_s.at[k], pp_r.at[k], partner)
                write_out(xx, 1 - core, wave, h)

    start_wave(0)
    relay_wave(0)
    start_wave(1)

    gq_t = jnp.dot(keys_t[...], grads[...], preferred_element_type=F32)
    gq_out[:, :, :vd] = gq_t[:vd].T.astype(BF16).reshape(CTX, per, vd)
    gq_out[:, :, vd:] = gq_t[vd:].T.astype(BF16).reshape(CTX, per, width - vd)

    def send_gq(k, carry):
        to = (ctx + k) % CTX
        remote(gq_out.at[to], gq_in.at[k], gq_s.at[k], gq_r.at[k], (to, head)).start()
        return carry

    lax.fori_loop(1, CTX, send_gq, 0)

    relay_wave(1)
    finish_wave(0)
    for way in range(2):
        from_side(0, way, way)
    finish_wave(1)
    for way in range(2):
        from_side(0, way, 1 - way)
    for way in range(2):
        from_side(1, way, way)

    def add_att(k, total):
        remote(att_in.at[k], att_in.at[k], at_s.at[k], at_r.at[k], ((ctx + k) % CTX, head)).wait_recv()
        return total + att_in[k].astype(F32)

    att_ref[...] = lax.fori_loop(1, CTX, add_att, att_out[ctx].astype(F32)).astype(BF16)

    def add_gq(k, total):
        remote(gq_in.at[k], gq_in.at[k], gq_s.at[k], gq_r.at[k], ((ctx + k) % CTX, head)).wait_recv()
        return total + gq_in[k].astype(F32)

    grad_query = lax.fori_loop(1, CTX, add_gq, gq_out[ctx].astype(F32))
    rotary = grad_query[:, vd:]
    gq_ref[:, :vd] = grad_query[:, :vd]
    gq_ref[:, vd:] = rotary * cosines - swapped(rotary) * signed

    for way in range(2):
        from_far(0, way)
    for way in range(2):
        from_side(1, way, 1 - way)
    for way in range(2):
        from_far(1, way)
    from_partner(0)
    from_partner(1)

    def drain(k, carry):
        to = (ctx + k) % CTX
        remote(att_out.at[to], att_in.at[k], at_s.at[k], at_r.at[k], (to, head)).wait_send()
        remote(gq_out.at[to], gq_in.at[k], gq_s.at[k], gq_r.at[k], (to, head)).wait_send()
        return carry

    lax.fori_loop(1, CTX, drain, 0)
    for copy in sends:
        copy.wait_send()
    for copy in landed:
        copy.wait()


def rotation_tables(half_width):
    frequency = 10000.0 ** (-np.arange(half_width) / half_width)
    angles = np.outer(2.0 ** np.arange(position_bits), frequency)
    angles = np.concatenate([angles, angles], axis=1)
    return np.cos(angles).astype(np.float32), np.sin(angles).astype(np.float32)


def body(query, cache, cotangent, positions, visible):
    _, per, width = query.shape
    vd = cotangent.shape[-1]
    n_keys = cache.shape[0]
    rows = CTX * per
    wave_keys = n_keys // HEAD // 2
    half_keys = wave_keys // 2
    cos_table, sin_table = rotation_tables((width - vd) // 2)
    vmem = pl.BlockSpec(memory_space=pltpu.VMEM)
    smem = pl.BlockSpec(memory_space=pltpu.SMEM)
    hbm = pl.BlockSpec(memory_space=pl.ANY)
    V, dma = pltpu.VMEM, pltpu.SemaphoreType.DMA
    scratch = [
        V((SZ, SY, per, width), BF16),
        V((SZ, SY, per, vd), BF16),
        V((n_keys, width), BF16),
        V((width, n_keys), BF16),
        V((width, rows), BF16),
        V((vd, rows), BF16),
        V((2 * rows, vd), BF16),
        V((n_keys, rows), F32),
        V((n_keys, rows), F32),
        V((n_keys, rows), BF16),
        V((n_keys, rows), BF16),
        V((16, 128), F32),
        V((SY, 16, 128), F32),
        V((SZ, 16, 128), F32),
        V((8, wave_keys, width), F32),
        V((8, wave_keys, width), BF16),
        V((8, wave_keys, width), BF16),
        V((2, 2, half_keys, width), BF16),
        V((2, 2, half_keys, width), BF16),
        V((2, 2, 2, half_keys, width), BF16),
        V((2, 2, 2, half_keys, width), BF16),
        V((CTX, per, vd), BF16),
        V((CTX, per, vd), BF16),
        V((CTX, per, width), BF16),
        V((CTX, per, width), BF16),
        dma(()),
        dma((SY,)), dma((SY,)), dma((SZ * SY,)), dma((SZ * SY,)),
        dma((SZ,)), dma((SZ,)), dma((SY,)), dma((SY,)),
        dma((SY,)), dma((SY,)), dma((SZ,)), dma((SZ,)),
        dma((8,)), dma((8,)), dma((4,)), dma((4,)), dma((8,)), dma((8,)),
        dma((8,)), dma((8,)), dma((4,)), dma((4,)), dma((16,)), dma((16,)),
        dma((32,)),
        dma((CTX,)), dma((CTX,)), dma((CTX,)), dma((CTX,)),
    ]
    attention, grad_query, grad_cache = pl.pallas_call(
        kernel,
        out_shape=(
            jax.ShapeDtypeStruct((per, vd), BF16),
            jax.ShapeDtypeStruct((per, width), F32),
            jax.ShapeDtypeStruct((n_keys, width), BF16),
        ),
        in_specs=[smem, smem, vmem, vmem, vmem, vmem, hbm],
        out_specs=(vmem, vmem, hbm),
        scratch_shapes=scratch,
        compiler_params=pltpu.CompilerParams(
            collective_id=0, has_side_effects=True, vmem_limit_bytes=62 * 1024 * 1024
        ),
        name="latent_attention",
    )(
        visible,
        positions,
        jnp.asarray(cos_table),
        jnp.asarray(sin_table),
        query.reshape(per, width),
        cotangent.reshape(per, vd),
        cache,
    )
    return attention[None], grad_query[None], grad_cache


def solution(mesh):
    placed = (P("ctx", "head", None), P("ctx", None), P("ctx", "head", None), P("ctx"), P())
    return jax.shard_map(
        body,
        mesh=mesh,
        in_specs=placed,
        out_specs=(P("ctx", "head", None), P("ctx", "head", None), P("ctx", None)),
        check_vma=False,
    )
```

time: 326 us -> 123 us (0.38)
  blocking collectives: 124 us -> 0 us
  Pallas kernels: 0 us -> 104 us
  waiting for transfers between devices: 83.2 us -> 0 us
  matrix products: 42.9 us -> 0 us
  other arithmetic: 26.7 us -> 0 us
  starting transfers between devices: 26.2 us -> 0 us
  between operations: 15.3 us -> 1.3 us
  local copies, waits for them, and re-layouts: 6.96 us -> 16.5 us
    psum x1 -> x0, blocking collectives: 109 us -> none  [body(): grad_cache = lax.psum(grad_latent, 'head').astype(jnp.bfloat16)]
    pallas_call x0 -> x1, Pallas kernels: none -> 104 us  [body(): pl.pallas_call(kernel, out_shape=(jax.ShapeDtypeStruct((per, vd), BF16),...]
    all_gather x1 -> x0, waiting for transfers between devices: 74.6 us -> none  [gather_packed(): lines, at, gathered = (lax.all_gather(vector, axis), 0, [])]
    dot_general x6 -> x0, matrix products: 42.9 us -> none  [the longest x1 10.3 us: body(): jnp.einsum('thv,kv->thk', gradients, values, preferred_element_type=jnp.f...]
    all_to_all x4 -> x0, starting transfers between devices: 26.1 us -> none  [the longest x2 18.3 us: sent_and_summed(): lax.all_to_all(parts, axis, split_axis=0, concat_axis=0, tiled=True)]
    all_to_all x1 -> x0, blocking collectives: 14.7 us -> none  [from_everyone(): return lax.all_to_all(copies, axis, split_axis=0, concat_axis=0, tiled=True)]
    unnamed x17 -> x8, local copies, waits for them, and re-layouts: 3.04 us -> 16.5 us
    convert_element_type x2 -> x0, other arithmetic: 8.72 us -> none  [the longest x1 7.99 us: body(): (probs * (grad_probs - delta[..., None]) * softmax_scale).astype(jnp.bflo...]
  transfers between devices with their start and end apart: 5 -> 0, of which waited for: 2 -> 0; matrix products, arithmetic and copies ran while one was open for 11% -> 0% of each run, Pallas kernels for 0% -> 0%
where the time goes in v1:
time: 123 us; the launch traced here: 122 us
  Pallas kernels  104 us (85%)
  local copies, waits for them, and re-layouts  16.5 us (13%)
  between operations  1.3 us (1%)
    pallas_call x1, Pallas kernels, body(): pl.pallas_call(kernel, out_shape=(jax.ShapeDtypeStruct((per, vd), BF16),...  104 us
    unnamed x8, local copies, waits for them, and re-layouts  16.5 us

profile of v1, /device:TPU:1, one launch (start us, length us, event | category | flops | bytes accessed | tf_op | source)
XLA Modules:
  0.0 122.3 jit_solution(13618143177103890743)
XLA Ops:
  1.3 7.7 %copy.10.cache_ref = bf16[4096,576]{1,0:T(8,128)(2,1)} copy(bf16[4096,576]{0,1:T(8,128)(2,1)} %param.8) | data formatting | bytes 9437184 | tf_op args[1]
  8.9 104.5 %latent_attention.1 = (bf16[16,512]{1,0:T(8,128)(2,1)}, f32[16,576]{1,0:T(8,128)}, bf16[4096,576]{1,0:T(8,128)(2,1)}) custom-call(s32[32]{0:T(128)} %vis_ref.1, s32[1]{0:T(128)S(6)} %copy.14.pos_ref, f32[18,64]{1,0:T(8,128)} %constant.4.clone.cos_ref, f32[18,64]{1,0:T(8,128)} %constant.5.clone.sin_ref, bf16[16,576]{1,0:T(8,128)(2,1)} %bitcast.5, ...), custom_call_target="tpu_custom_call" | custom-call | tf_op jit(solution)/shard_map/latent_attention/pallas_call | solution.py:513
  113.4 0.0 copy-start.1
  113.4 0.0 copy-start
  113.4 7.7 %copy.11 = bf16[4096,576]{0,1:T(8,128)(2,1)} copy(bf16[4096,576]{1,0:T(8,128)(2,1)} %get-tuple-element.11) | data formatting | bytes 9437184
  121.1 0.0 copy-done.1
  121.1 0.6 copy.15
  121.7 0.0 copy-done
  121.7 0.6 copy.16
Async XLA Ops:
  113.4 7.7 %copy-start.1 = (bf16[16,512]{1,0:T(8,128)(2,1)S(1)}, bf16[16,512]{1,0:T(8,128)(2,1)}, u32[]{:S(2)}) copy-start(bf16[16,512]{1,0:T(8,128)(2,1)} %get-tuple-element.6) | copy-start | bytes 49156
  113.4 8.3 %copy-start = (f32[16,576]{1,0:T(8,128)S(1)}, f32[16,576]{1,0:T(8,128)}, u32[]{:S(2)}) copy-start(f32[16,576]{1,0:T(8,128)} %get-tuple-element.7) | copy-start | bytes 110596

commit v2 on v1

v2 whole, which is shorter than its diff:
```python
import jax
import jax.numpy as jnp
import numpy as np
from jax import lax
from jax.experimental import pallas as pl
from jax.experimental.pallas import tpu as pltpu
from jax.sharding import PartitionSpec as P

softmax_scale = 192.0 ** (-0.5)
log2_scale = softmax_scale * float(np.log2(np.e))
position_bits = 18
masked_value = -1e30

SZ, SY, SX = 8, 4, 4
CTX, HEAD = SZ * SY, SX * 2
F32, BF16 = jnp.float32, jnp.bfloat16
MESH = pl.DeviceIdType.MESH


def remote(src, dst, send_sem, recv_sem, device):
    return pltpu.make_async_remote_copy(
        src_ref=src,
        dst_ref=dst,
        send_sem=send_sem,
        recv_sem=recv_sem,
        device_id=device,
        device_id_type=MESH,
    )


def dot_nt(a, b):
    return lax.dot_general(a, b, (((1,), (1,)), ((), ())), preferred_element_type=F32)


def kernel(
    vis_ref, pos_ref, cos_ref, sin_ref, query_ref, cot_ref, cache_ref,
    att_ref, gq_ref, gc_ref,
    qb, dob, keys_t, qdo_t, qr_t, scores, gprobs, low,
    seen, seen_f, line_a, line_b, stat_own, stat_y, stat_z, acc, dd_out, dd_in, opp_out, opp_in, rs_out, rs_in,
    att_out, att_in, gq_out, gq_in,
    cache_sem, qy_s, qy_r, qz_s, qz_r, dz_s, dz_r, dy_s, dy_r,
    sy_s, sy_r, sz_s, sz_r, dd_s, dd_r, op_s, op_r, rs_s, rs_r,
    ag_s, ag_r, fw_s, fw_r, pp_s, pp_r, at_s, at_r, gq_s, gq_r,
):
    ctx = lax.axis_index("ctx")
    head = lax.axis_index("head")
    z, y = ctx // SY, ctx % SY
    x, core = head // 2, head % 2
    n_keys = keys_t.shape[1]
    vd = cot_ref.shape[2]
    width = query_ref.shape[2]
    per = query_ref.shape[1]
    rows = CTX * per
    own_keys = n_keys // HEAD
    wave_keys = own_keys // 2
    half_keys = wave_keys // 2
    sends = []

    def plane(zz, yy):
        return (zz % SZ) * SY + yy % SY, head

    right = (ctx, ((x + 1) % SX) * 2 + core)
    left = (ctx, ((x + SX - 1) % SX) * 2 + core)
    partner = (ctx, x * 2 + 1 - core)

    def send(*args):
        copy = remote(*args)
        copy.start()
        sends.append(copy)

    def arrive(dst, send_sem, recv_sem, device):
        remote(dst, dst, send_sem, recv_sem, device).wait_recv()

    load = pltpu.make_async_copy(cache_ref, keys_t, cache_sem)
    load.start()

    barrier = pltpu.get_barrier_semaphore()

    def greet(k, carry):
        pl.semaphore_signal(
            barrier, inc=1, device_id=((ctx + k) % CTX, head), device_id_type=MESH
        )
        return carry

    lax.fori_loop(1, CTX, greet, 0)
    for device in (right, left, partner):
        pl.semaphore_signal(barrier, inc=1, device_id=device, device_id_type=MESH)

    position = pos_ref[0]
    half = (width - vd) // 2
    cosines = jnp.ones((1, 2 * half), F32)
    sines = jnp.zeros((1, 2 * half), F32)
    for bit in range(position_bits):
        switch = ((position >> bit) & 1).astype(F32)
        step_cos = 1.0 + switch * (cos_ref[bit : bit + 1, :] - 1.0)
        step_sin = switch * sin_ref[bit : bit + 1, :]
        cosines, sines = (
            cosines * step_cos - sines * step_sin,
            sines * step_cos + cosines * step_sin,
        )
    lower = lax.broadcasted_iota(jnp.int32, (1, 2 * half), 1) < half
    signed = jnp.where(lower, -sines, sines)

    def swapped(t):
        return jnp.concatenate([t[:, half:], t[:, :half]], axis=1)

    rotary = query_ref[0, :, vd:].astype(F32)
    qb[z, y, :, :vd] = query_ref[0, :, :vd]
    qb[z, y, :, vd:] = (rotary * cosines + swapped(rotary) * signed).astype(BF16)
    dob[z, y] = cot_ref[0]

    for t in range(CTX):
        seen[t * per : (t + 1) * per, :] = jnp.full((per, 128), vis_ref[t], jnp.int32)

    pl.semaphore_wait(barrier, CTX - 1 + 3)

    for d in range(1, SY):
        send(qb.at[z, y], qb.at[z, y], qy_s.at[d], qy_r.at[d], plane(z, y + d))
    for d in range(1, SZ):
        send(dob.at[z, y], dob.at[z, y], dz_s.at[d], dz_r.at[d], plane(z + d, y))

    def ring(way, step, d):
        sign = 1 if way == 0 else -1
        zz = (z - sign * (step - 1) + SZ) % SZ
        yy = (y - d + SY) % SY
        at = (way * (SZ // 2) + step - 1) * SY + d
        block = qb.at[zz, yy]
        send(block, block, qz_s.at[at], qz_r.at[at], plane(z + sign + SZ, y))

    def ring_arrive(way, step, d):
        sign = 1 if way == 0 else -1
        zz = (z - sign * step + SZ) % SZ
        yy = (y - d + SY) % SY
        at = (way * (SZ // 2) + step - 1) * SY + d
        arrive(qb.at[zz, yy], qz_s.at[at], qz_r.at[at], plane(z + sign + SZ, y))

    def carried(way, step, d):
        return step < SZ // 2 or (d < SY // 2) == (way == 0)

    for d in range(SY):
        if d:
            src = qb.at[z, (y - d + SY) % SY]
            arrive(src, qy_s.at[d], qy_r.at[d], plane(z, y + d))
        ring(0, 1, d)
        ring(1, 1, d)
    for step in range(1, SZ // 2 + 1):
        for d in range(SY):
            for way in range(2):
                if carried(way, step, d):
                    ring_arrive(way, step, d)
                    if step < SZ // 2 and carried(way, step + 1, d):
                        ring(way, step + 1, d)
        if step == 2:
            for d in range(1, SZ):
                src = dob.at[(z - d + SZ) % SZ, y]
                arrive(src, dz_s.at[d], dz_r.at[d], plane(z + d, y))
            for d in range(1, SY):
                src = dob.at[:, y]
                send(src, src, dy_s.at[d], dy_r.at[d], plane(z, y + d))

    load.wait()
    chunk = 256
    n_chunks = n_keys // chunk
    first_key = ctx * n_keys
    line_a[...] = jnp.full(line_a.shape, 2 * masked_value, F32)

    def score(i, carry):
        at = pl.multiple_of(i * chunk, chunk)
        raw = jnp.dot(
            qb[...].reshape(rows, width), keys_t[:, pl.ds(at, chunk)], preferred_element_type=F32
        )
        top = line_a[...]
        for part in range(chunk // 128):
            spot_at = pl.multiple_of(at + part * 128, 128)
            piece = raw[:, part * 128 : (part + 1) * 128] * log2_scale
            piece = jnp.where(first_key + spot_at < seen[...], piece, masked_value)
            scores[:, pl.ds(spot_at, 128)] = piece
            top = jnp.maximum(top, piece)
        line_a[...] = top
        return carry

    lax.fori_loop(0, n_chunks, score, 0)
    peak = jnp.max(line_a[...], axis=1, keepdims=True)
    peak_line = line_b
    peak_line[...] = jnp.broadcast_to(peak, peak_line.shape)

    for d in range(1, SY):
        src = dob.at[:, (y - d + SY) % SY]
        arrive(src, dy_s.at[d], dy_r.at[d], plane(z, y + d))

    mass_line, inner_line = line_a, seen_f
    mass_line[...] = jnp.zeros(line_a.shape, F32)
    inner_line[...] = jnp.zeros(line_a.shape, F32)

    def weigh(i, carry):
        at = pl.multiple_of(i * chunk, chunk)
        gp = jnp.dot(
            dob[...].reshape(rows, vd), keys_t[:vd, pl.ds(at, chunk)], preferred_element_type=F32
        )
        gprobs[:, pl.ds(at, chunk)] = gp
        mass, inner = mass_line[...], inner_line[...]
        for part in range(chunk // 128):
            window = pl.ds(pl.multiple_of(at + part * 128, 128), 128)
            weights = jnp.exp2(scores[:, window] - peak_line[...])
            scores[:, window] = weights
            low[:, window] = weights.astype(BF16)
            mass = mass + weights
            inner = inner + weights * gp[:, part * 128 : (part + 1) * 128]
        mass_line[...] = mass
        inner_line[...] = inner
        return carry

    lax.fori_loop(0, n_chunks, weigh, 0)
    mass = jnp.sum(mass_line[...], axis=1, keepdims=True)
    inner = jnp.sum(inner_line[...], axis=1, keepdims=True)
    lanes = lax.broadcasted_iota(jnp.int32, (rows, 128), 1)
    table = jnp.where(lanes == 0, peak, jnp.where(lanes == 1, mass, inner)).T
    peak, mass, inner = (table[i : i + 1, :] for i in range(3))

    n_lines = rows // 128

    def put_stats(ref, stats):
        for k, stat in enumerate(stats):
            for i in range(n_lines):
                ref[k * n_lines + i : k * n_lines + i + 1, :] = stat[:, i * 128 : (i + 1) * 128]

    def merge(parts):
        tops = [p[:n_lines] for p in parts]
        best = tops[0]
        for t in tops[1:]:
            best = jnp.maximum(best, t)
        total, dots = 0.0, 0.0
        for t, p in zip(tops, parts):
            factor = jnp.exp2(t - best)
            total = total + factor * p[n_lines : 2 * n_lines]
            dots = dots + factor * p[2 * n_lines : 3 * n_lines]
        return best, total, dots

    put_stats(stat_own, (peak, mass, inner, jnp.zeros_like(peak)))
    for d in range(1, SY):
        send(stat_own, stat_y.at[d], sy_s.at[d], sy_r.at[d], plane(z, y + d))
    first = dot_nt(low[: rows // 2, :], keys_t[:vd, :])
    for d in range(1, SY):
        arrive(stat_y.at[d], sy_s.at[d], sy_r.at[d], plane(z, y + d))
    best, total, dots = merge([stat_own[...]] + [stat_y[d] for d in range(1, SY)])
    stat_z[0, :n_lines] = best
    stat_z[0, n_lines : 2 * n_lines] = total
    stat_z[0, 2 * n_lines : 3 * n_lines] = dots
    stat_z[0, 3 * n_lines :] = jnp.zeros_like(dots)
    for d in range(1, SZ):
        send(stat_z.at[0], stat_z.at[d], sz_s.at[d], sz_r.at[d], plane(z + d, y))
    second = dot_nt(low[rows // 2 :, :], keys_t[:vd, :])
    attended = jnp.concatenate([first, second], axis=0)
    q_all = qb[...].reshape(rows, width)
    qdo_t[:, :rows] = q_all[:, :vd].T
    qdo_t[:, rows:] = dob[...].reshape(rows, vd).T
    qr_t[...] = q_all[:, vd:].T
    for d in range(1, SZ):
        arrive(stat_z.at[d], sz_s.at[d], sz_r.at[d], plane(z + d, y))
    best, total, dots = merge([stat_z[d] for d in range(SZ)])

    def across(v):
        return jnp.concatenate([v[i : i + 1, :] for i in range(n_lines)], axis=1)

    def down(v):
        return jnp.broadcast_to(v, (128, rows)).T

    factor, delta = line_a, line_b
    factor[...] = down(jnp.exp2(peak - across(best)) / across(total))
    delta[...] = down(across(dots) / across(total))

    for i in range(vd // 128):
        cols = slice(i * 128, (i + 1) * 128)
        block = attended[:, cols] * factor[...]
        att_out[:, :, cols] = block.astype(BF16).reshape(CTX, per, 128)

    def send_att(k, carry):
        to = (ctx + k) % CTX
        remote(att_out.at[to], att_in.at[k], at_s.at[k], at_r.at[k], (to, head)).start()
        return carry

    def spot(xx, cc, wave):
        return pl.multiple_of((xx * 2 + cc) * own_keys + wave * wave_keys, wave_keys)

    def terms(at):
        grad, probs = [], []
        for part in range(wave_keys // 128):
            window = pl.ds(pl.multiple_of(at + part * 128, 128), 128)
            prob = scores[:, window] * factor[...]
            grad.append((prob * (gprobs[:, window] - delta[...]) * softmax_scale).astype(BF16))
            probs.append(prob.astype(BF16))
        grad = jnp.concatenate(grad, axis=1)
        low[:, pl.ds(at, wave_keys)] = grad
        both = jnp.concatenate([grad, jnp.concatenate(probs, axis=1)], axis=0)
        value = jnp.dot(qdo_t[...], both, preferred_element_type=F32)
        return value, jnp.dot(qr_t[...], grad, preferred_element_type=F32)

    offsets = (2, 1, 3, 0)
    halves = (slice(0, half_keys), slice(half_keys, 2 * half_keys))

    def chip_sum(wave, slot, part):
        at = wave * 4 + slot
        return acc[at, :, part] + dd_in[at, :, part].astype(F32)

    def start_wave(wave):
        for slot, offset in enumerate(offsets):
            if slot == 3:
                relay_wave(wave)
            at = wave * 4 + slot
            xx = (x + offset) % SX
            value, rotary_part = terms(spot(xx, 1 - core, wave))
            dd_out[at, :vd, :] = value.astype(BF16)
            dd_out[at, vd:, :] = rotary_part.astype(BF16)
            send(dd_out.at[at], dd_in.at[at], dd_s.at[at], dd_r.at[at], partner)
            value, rotary_part = terms(spot(xx, core, wave))
            acc[at, :vd, :] = value
            acc[at, vd:, :] = rotary_part
            arrive(dd_in.at[at], dd_s.at[at], dd_r.at[at], partner)
            if slot == 0:
                if wave == 0:
                    lax.fori_loop(1, CTX, send_att, 0)
                for h, device in ((0, right), (1, left)):
                    opp_out[wave, h] = chip_sum(wave, 0, halves[h]).astype(BF16)
                    k = wave * 2 + h
                    send(opp_out.at[wave, h], opp_in.at[wave, h], op_s.at[k], op_r.at[k], device)
            if slot == 1:
                send_rs(wave, 0, 1, None)
            if slot == 2:
                send_rs(wave, 1, 0, None)

    def send_rs(wave, way, h, extra):
        part = chip_sum(wave, 1 + way, halves[h])
        if extra is not None:
            part = part + extra.astype(F32)
        rs_out[wave, way, h] = part.astype(BF16)
        k = (wave * 2 + way) * 2 + h
        device = (right, left)[way]
        send(rs_out.at[wave, way, h], rs_in.at[wave, way, h], rs_s.at[k], rs_r.at[k], device)

    def relay_wave(wave):
        for h, device in ((0, right), (1, left)):
            k = wave * 2 + h
            arrive(opp_in.at[wave, h], op_s.at[k], op_r.at[k], device)
            send_rs(wave, h, h, opp_in[wave, h])

    full = gc_ref

    def piece(xx, cc, wave, h):
        return (xx * 2 + cc) * 4 + wave * 2 + h

    def finish_wave(wave):
        for h in range(2):
            for way in range(2):
                k = (wave * 2 + way) * 2 + h
                arrive(rs_in.at[wave, way, h], rs_s.at[k], rs_r.at[k], (right, left)[way])
        for h in range(2):
            done = chip_sum(wave, 3, halves[h])
            done = done + rs_in[wave, 0, h].astype(F32) + rs_in[wave, 1, h].astype(F32)
            full[piece(x, core, wave, h)] = done.astype(BF16)
        for h, way in ((0, 0), (1, 1), (1, 0), (0, 1)):
            src = full.at[piece(x, core, wave, h)]
            k = (wave * 2 + way) * 2 + h
            send(src, src, ag_s.at[k], ag_r.at[k], (right, left)[way])
        for h in range(2):
            to_partner(0, x, wave, h)

    def to_partner(kind, xx, wave, h):
        src = full.at[piece(xx, core, wave, h)]
        k = (kind * 2 + wave) * 2 + h
        send(src, src, pp_s.at[k], pp_r.at[k], partner)

    def from_side(wave, way, h):
        xx = (x + (SX - 1 if way == 0 else 1)) % SX
        here = full.at[piece(xx, core, wave, h)]
        k = (wave * 2 + way) * 2 + h
        arrive(here, ag_s.at[k], ag_r.at[k], (right, left)[way])
        if h == way:
            k = wave * 2 + way
            send(here, here, fw_s.at[k], fw_r.at[k], (right, left)[way])
        to_partner(1 + way, xx, wave, h)

    def from_far(wave, way):
        xx = (x + 2) % SX
        here = full.at[piece(xx, core, wave, way)]
        k = wave * 2 + way
        arrive(here, fw_s.at[k], fw_r.at[k], (right, left)[way])
        to_partner(3, xx, wave, way)

    def from_partner(wave):
        for kind, offset in enumerate((0, 3, 1, 2)):
            for h in range(2):
                xx = (x + offset) % SX
                here = full.at[piece(xx, 1 - core, wave, h)]
                k = (kind * 2 + wave) * 2 + h
                arrive(here, pp_s.at[k], pp_r.at[k], partner)

    start_wave(0)
    start_wave(1)
    finish_wave(0)

    grad_rotated = dot_nt(low[...], keys_t[...])
    gq_out[...] = grad_rotated.astype(BF16).reshape(CTX, per, width)

    def send_gq(k, carry):
        to = (ctx + k) % CTX
        remote(gq_out.at[to], gq_in.at[k], gq_s.at[k], gq_r.at[k], (to, head)).start()
        return carry

    lax.fori_loop(1, CTX, send_gq, 0)

    for way in range(2):
        from_side(0, way, way)
    finish_wave(1)
    for way in range(2):
        from_side(0, way, 1 - way)
    for way in range(2):
        from_side(1, way, way)

    def add_att(k, total):
        remote(att_in.at[k], att_in.at[k], at_s.at[k], at_r.at[k], ((ctx + k) % CTX, head)).wait_recv()
        return total + att_in[k].astype(F32)

    att_ref[0] = lax.fori_loop(1, CTX, add_att, att_out[ctx].astype(F32)).astype(BF16)

    def add_gq(k, total):
        remote(gq_in.at[k], gq_in.at[k], gq_s.at[k], gq_r.at[k], ((ctx + k) % CTX, head)).wait_recv()
        return total + gq_in[k].astype(F32)

    grad_query = lax.fori_loop(1, CTX, add_gq, gq_out[ctx].astype(F32))
    rotary = grad_query[:, vd:]
    gq_ref[0, :, :vd] = grad_query[:, :vd]
    gq_ref[0, :, vd:] = rotary * cosines - swapped(rotary) * signed

    for way in range(2):
        from_far(0, way)
    for way in range(2):
        from_side(1, way, 1 - way)
    for way in range(2):
        from_far(1, way)
    from_partner(0)
    from_partner(1)

    def drain(k, carry):
        to = (ctx + k) % CTX
        remote(att_out.at[to], att_in.at[k], at_s.at[k], at_r.at[k], (to, head)).wait_send()
        remote(gq_out.at[to], gq_in.at[k], gq_s.at[k], gq_r.at[k], (to, head)).wait_send()
        return carry

    lax.fori_loop(1, CTX, drain, 0)
    for copy in sends:
        copy.wait_send()


def put_out(att_held, gq_held, gc_held, att_ref, gq_ref, gc_ref, sems):
    pieces = gc_held.shape[0]
    copies = [
        pltpu.make_async_copy(gc_held.at[i], gc_ref.at[:, i * 128 : (i + 1) * 128], sems.at[i])
        for i in range(pieces)
    ]
    copies.append(pltpu.make_async_copy(att_held, att_ref, sems.at[pieces]))
    copies.append(pltpu.make_async_copy(gq_held, gq_ref, sems.at[pieces + 1]))
    for copy in copies:
        copy.start()
    for copy in copies:
        copy.wait()


def rotation_tables(half_width):
    frequency = 10000.0 ** (-np.arange(half_width) / half_width)
    angles = np.outer(2.0 ** np.arange(position_bits), frequency)
    angles = np.concatenate([angles, angles], axis=1)
    return np.cos(angles).astype(np.float32), np.sin(angles).astype(np.float32)


def body(query, cache, cotangent, positions, visible):
    _, per, width = query.shape
    vd = cotangent.shape[-1]
    n_keys = cache.shape[0]
    rows = CTX * per
    wave_keys = n_keys // HEAD // 2
    half_keys = wave_keys // 2
    cos_table, sin_table = rotation_tables((width - vd) // 2)
    vmem = pl.BlockSpec(memory_space=pltpu.VMEM)
    smem = pl.BlockSpec(memory_space=pltpu.SMEM)
    hbm = pl.BlockSpec(memory_space=pl.ANY)
    V, dma = pltpu.VMEM, pltpu.SemaphoreType.DMA
    scratch = [
        V((SZ, SY, per, width), BF16),
        V((SZ, SY, per, vd), BF16),
        V((width, n_keys), BF16),
        V((vd, 2 * rows), BF16),
        V((width - vd, rows), BF16),
        V((rows, n_keys), F32),
        V((rows, n_keys), F32),
        V((rows, n_keys), BF16),
        V((rows, 128), jnp.int32),
        V((rows, 128), F32),
        V((rows, 128), F32),
        V((rows, 128), F32),
        V((16, 128), F32),
        V((SY, 16, 128), F32),
        V((SZ, 16, 128), F32),
        V((8, width, wave_keys), F32),
        V((8, width, wave_keys), BF16),
        V((8, width, wave_keys), BF16),
        V((2, 2, width, half_keys), BF16),
        V((2, 2, width, half_keys), BF16),
        V((2, 2, 2, width, half_keys), BF16),
        V((2, 2, 2, width, half_keys), BF16),
        V((CTX, per, vd), BF16),
        V((CTX, per, vd), BF16),
        V((CTX, per, width), BF16),
        V((CTX, per, width), BF16),
        dma(()),
        dma((SY,)), dma((SY,)), dma((SZ * SY,)), dma((SZ * SY,)),
        dma((SZ,)), dma((SZ,)), dma((SY,)), dma((SY,)),
        dma((SY,)), dma((SY,)), dma((SZ,)), dma((SZ,)),
        dma((8,)), dma((8,)), dma((4,)), dma((4,)), dma((8,)), dma((8,)),
        dma((8,)), dma((8,)), dma((4,)), dma((4,)), dma((16,)), dma((16,)),
        dma((CTX,)), dma((CTX,)), dma((CTX,)), dma((CTX,)),
    ]
    pieces = n_keys // 128
    held = (
        V((1, per, vd), BF16),
        V((1, per, width), F32),
        V((pieces, width, 128), BF16),
    )
    held = pl.pallas_call(
        kernel,
        out_shape=held,
        in_specs=[smem, smem, vmem, vmem, vmem, vmem, hbm],
        out_specs=(vmem, vmem, vmem),
        scratch_shapes=scratch,
        compiler_params=pltpu.CompilerParams(
            collective_id=0, has_side_effects=True, vmem_limit_bytes=56 * 1024 * 1024
        ),
        name="latent_attention",
    )(
        visible,
        positions,
        jnp.asarray(cos_table),
        jnp.asarray(sin_table),
        query,
        cotangent,
        cache.T,
    )
    attention, grad_query, grad_cache = pl.pallas_call(
        put_out,
        out_shape=(
            jax.ShapeDtypeStruct((1, per, vd), BF16),
            jax.ShapeDtypeStruct((1, per, width), F32),
            jax.ShapeDtypeStruct((width, n_keys), BF16),
        ),
        in_specs=[hbm, hbm, hbm],
        out_specs=(hbm, hbm, hbm),
        scratch_shapes=[dma((pieces + 2,))],
        compiler_params=pltpu.CompilerParams(vmem_limit_bytes=1024 * 1024),
        name="put_out",
    )(*held)
    return attention, grad_query, grad_cache.T


def solution(mesh):
    placed = (P("ctx", "head", None), P("ctx", None), P("ctx", "head", None), P("ctx"), P())
    return jax.shard_map(
        body,
        mesh=mesh,
        in_specs=placed,
        out_specs=(P("ctx", "head", None), P("ctx", "head", None), P("ctx", None)),
        check_vma=False,
    )
```

time: 123 us -> 104 us (0.85)
  local copies, waits for them, and re-layouts: 16.5 us -> 0 us
  Pallas kernels: 104 us -> 102 us
    unnamed x8 -> x0, local copies, waits for them, and re-layouts: 16.5 us -> none
    pallas_call x1 -> x2, Pallas kernels: 104 us -> 102 us  [the longest x1 99.6 us: body(): pl.pallas_call(kernel, out_shape=held, in_specs=[smem, smem, vmem, vmem,...]
where the time goes in v2:
time: 104 us; the launch traced here: 103 us
  Pallas kernels  102 us (98%)
  between operations  1.45 us (1%)
    pallas_call x1, Pallas kernels, body(): pl.pallas_call(kernel, out_shape=held, in_specs=[smem, smem, vmem, vmem,...  99.6 us
    pallas_call x1, Pallas kernels, body(): pl.pallas_call(put_out, out_shape=(jax.ShapeDtypeStruct((1, per, vd), BF1...  2.47 us

profile of v2, /device:TPU:1, one launch (start us, length us, event | category | flops | bytes accessed | tf_op | source)
XLA Modules:
  0.0 103.5 jit_solution(2843292750077234736)
XLA Ops:
  1.3 99.6 %latent_attention.1 = (bf16[1,16,512]{2,1,0:T(8,128)(2,1)S(1)}, f32[1,16,576]{2,1,0:T(8,128)S(1)}, bf16[32,576,128]{2,1,0:T(8,128)(2,1)S(1)}) custom-call(s32[32]{0:T(128)} %vis_ref.1, s32[1]{0:T(128)S(6)} %copy.10.pos_ref, f32[18,64]{1,0:T(8,128)} %constant.4.clone.cos_ref, f32[18,64]{1,0:T(8,128)} %constant.5.clone.sin_ref, bf16[1,16,576]{2,1,0:T(8,128)(2,1)} %query_ref.1, ...), custom_call_target="tpu_custom_call" | custom-call | tf_op jit(solution)/shard_map/latent_attention/pallas_call | solution.py:528
  100.8 2.5 %put_out.1 = (bf16[1,16,512]{2,1,0:T(8,128)(2,1)}, f32[1,16,576]{2,1,0:T(8,128)}, bf16[576,4096]{1,0:T(8,128)(2,1)}) custom-call(bf16[1,16,512]{2,1,0:T(8,128)(2,1)S(1)} %get-tuple-element.9.att_held, f32[1,16,576]{2,1,0:T(8,128)S(1)} %get-tuple-element.10.gq_held, bf16[32,576,128]{2,1,0:T(8,128)(2,1)S(1)} %get-tuple-element.11.gc_held), custom_call_target="tpu_custom_call" | custom-call | tf_op jit(solution)/shard_map/put_out/pallas_call | solution.py:547
